TPU v7x, 32 devices: a whole 2x2x4 slice. The times are simulated.
32 devices in a mesh: dp: 4 (over z), expert: 8 (over y, x, core).
Axes of the slice: x: 2, y: 2, z: 4, core: 2. Of those that a mesh axis runs over, the one named last changes fastest.
Arguments:
- tokens: bfloat16 [2048, 2048], P(('dp', 'expert')), may hold values from -6 to 6
- norm_gain: bfloat16 [2048], replicated, may hold values from 0.099609375 to 1.8984375
- router_weight: bfloat16 [2048, 8], replicated, may hold values from -0.125 to 0.125
- gate_weight: bfloat16 [8, 2048, 5120], P('expert', None, 'dp'), may hold values from -0.125 to 0.125
- up_weight: bfloat16 [8, 2048, 5120], P('expert', None, 'dp'), may hold values from -0.125 to 0.125
- down_weight: bfloat16 [8, 5120, 2048], P('expert', 'dp'), may hold values from -0.078125 to 0.078125
- expert_picks: int32 [4, 8, 128], P('dp'), may hold values from 0 to 511, as said below
- final_gain: bfloat16 [2048], replicated, may hold values from 0.099609375 to 1.8984375
- kv_weight: bfloat16 [2048, 8, 6, 2, 64], P(None, 'expert'), may hold values from -0.125 to 0.125
Outputs:
- moe_out: bfloat16 [2048, 2048], P(('dp', 'expert'))
- kv_cache: bfloat16 [2048, 8, 6, 2, 64], P('dp', 'expert')
Inputs may be any that keep to these rules, and one draw needn't show every extreme that they name: `expert_picks`: for each group and expert, 128 different positions in the group. Of the 64 tokens of one device (positions s * 64 to (s + 1) * 64 - 1) one expert picks at most 32, and for every group and expert some device's tokens are picked exactly 32 times.
All inputs are finite; a program needn't handle non-finite values.
Results may differ from a plain program's by a relative error of at most 0.013.
Values may be sent and summed in bfloat16 or wider, within the bound.
A program may use at most 128 MiB of HBM per device.

v0:
```python
import jax
import jax.numpy as jnp
from jax import lax
from jax.sharding import PartitionSpec as P


def normalize(values, gain):
    return (
        values
        * lax.rsqrt(jnp.mean(values * values, axis=-1, keepdims=True) + 1e-06)
        * gain.astype(jnp.float32)
    )


def local(
    tokens,
    norm_gain,
    router_weight,
    gate_weight,
    up_weight,
    down_weight,
    expert_picks,
    final_gain,
    kv_weight,
):
    expert_count = lax.axis_size("expert")
    own_index = lax.axis_index("expert")
    tok_rows = tokens.shape[0]
    wide_tokens = tokens.astype(jnp.float32)
    normed = normalize(wide_tokens, norm_gain).astype(jnp.bfloat16)
    gate_probs = jax.nn.sigmoid(jnp.dot(normed, router_weight, preferred_element_type=jnp.float32))
    chosen = expert_picks[0]
    capacity = chosen.shape[1]
    slot_count = 4 * tok_rows // expert_count
    source = chosen // tok_rows
    local_row = chosen % tok_rows
    positions = jnp.arange(capacity, dtype=jnp.int32)
    earlier = (source[:, :, None] == source[:, None, :]) & (
        positions[None, None, :] < positions[None, :, None]
    )
    slot_rank = jnp.sum(earlier.astype(jnp.int32), axis=2)
    slot_ids = jnp.arange(slot_count, dtype=jnp.int32)
    shard_ids = jnp.arange(expert_count, dtype=jnp.int32)
    own_source = lax.dynamic_index_in_dim(source, own_index, 0, keepdims=False)
    own_rank = lax.dynamic_index_in_dim(slot_rank, own_index, 0, keepdims=False)
    compact_map = (
        (own_source[:, None, None] == shard_ids[None, :, None])
        & (own_rank[:, None, None] == slot_ids[None, None, :])
    ).astype(jnp.bfloat16)
    send_slot = (
        (source == own_index)[:, :, None] & (slot_rank[:, :, None] == slot_ids[None, None, :])
    ).astype(jnp.bfloat16)
    local_map = (
        local_row[:, :, None] == jnp.arange(tok_rows, dtype=jnp.int32)[None, None, :]
    ).astype(jnp.bfloat16)
    send_map = jnp.einsum("ecm,ect->emt", send_slot, local_map, preferred_element_type=jnp.float32)
    outgoing = jnp.einsum(
        "emt,td->emd", send_map.astype(jnp.bfloat16), normed, preferred_element_type=jnp.float32
    ).astype(jnp.bfloat16)
    incoming = lax.all_to_all(outgoing, "expert", split_axis=0, concat_axis=0, tiled=True)
    picked = jnp.einsum(
        "csm,smd->cd", compact_map, incoming, preferred_element_type=jnp.float32
    ).astype(jnp.bfloat16)
    gate_proj = gate_weight[0]
    up_proj = up_weight[0]
    down_proj = down_weight[0]
    block_rows = lax.all_gather(picked, "dp", axis=0, tiled=True)
    gate_act = jnp.dot(block_rows, gate_proj, preferred_element_type=jnp.float32)
    up_act = jnp.dot(block_rows, up_proj, preferred_element_type=jnp.float32)
    hidden_all = (jax.nn.gelu(gate_act, approximate=True) * up_act).astype(jnp.bfloat16)
    summed = lax.psum_scatter(
        jnp.dot(hidden_all, down_proj, preferred_element_type=jnp.float32).astype(jnp.bfloat16),
        "dp",
        scatter_dimension=0,
        tiled=True,
    )
    outbound = jnp.einsum(
        "csm,cd->smd", compact_map, summed, preferred_element_type=jnp.float32
    ).astype(jnp.bfloat16)
    returned = lax.all_to_all(outbound, "expert", split_axis=0, concat_axis=0, tiled=True)
    combine_weight = jnp.transpose(send_map, (2, 0, 1)) * gate_probs[:, :, None]
    combined = jnp.einsum(
        "tem,emd->td", combine_weight, returned.astype(jnp.float32), precision=lax.Precision.HIGHEST
    )
    moe_out = (wide_tokens + combined).astype(jnp.bfloat16)
    encoded = normalize(moe_out.astype(jnp.float32), final_gain).astype(jnp.bfloat16)
    kv_matrix = kv_weight.reshape(kv_weight.shape[0], -1)
    kv_rows = jnp.dot(
        lax.all_gather(encoded, "expert", axis=0, tiled=True),
        kv_matrix,
        preferred_element_type=jnp.float32,
    ).astype(jnp.bfloat16)
    kv_cache = kv_rows.reshape((kv_rows.shape[0],) + kv_weight.shape[1:])
    return (moe_out, kv_cache)


def solution(mesh):
    in_specs = (
        P(("dp", "expert"), None),
        P(),
        P(),
        P("expert", None, "dp"),
        P("expert", None, "dp"),
        P("expert", "dp", None),
        P("dp", None, None),
        P(),
        P(None, "expert", None, None, None),
    )
    out_specs = (P(("dp", "expert"), None), P("dp", "expert", None, None, None))
    return jax.shard_map(local, mesh=mesh, in_specs=in_specs, out_specs=out_specs, check_vma=False)
```

profile of v0, /device:TPU:0, one launch (start us, length us, event | category | flops | bytes accessed | tf_op | source)
XLA Modules:
  0.0 211.0 jit_solution(8727755176442680095)
XLA Ops:
  7.2 0.0 copy-start
  7.2 0.8 add_select_fusion
  8.1 0.8 broadcast_compare_fusion
  8.8 0.7 convert_element_type.51
  9.5 1.1 fusion.35
  10.6 0.0 copy-start.5
  10.6 0.4 convert_reduce_fusion
  11.0 0.2 fusion.40
  11.2 2.5 %convolution_convert_fusion.1 = bf16[8,32,2048]{2,1,0:T(8,128)(2,1)} fusion(bf16[64,2048]{1,0:T(8,128)(2,1)} %param.9, f32[2048]{0:T(1024)S(1)} %convert_element_type.51, f32[64]{0:T(128)S(1)} %add_rsqrt_fusion.1, f32[8,32,64]{2,1,0:T(8,128)S(1)} %fusion.40), kind=kOutput, calls=%fused_computation.18 | convolution fusion | flops 68173824 | bytes 1384704 | tf_op jit(solution)/shard_map/emt,td->emd/dot_general | solution.py:57
  13.7 5.2 %all-to-all-start = ((bf16[8,32,2048]{2,1,0:T(8,128)(2,1)}), bf16[8,32,2048]{2,1,0:T(8,128)(2,1)}, u32[]{:S(2)}, u32[]{:S(2)}) async-start(bf16[8,32,2048]{2,1,0:T(8,128)(2,1)} %convolution_convert_fusion.1), calls=%async_computation | async-start | bytes 2097152 | tf_op jit(solution)/shard_map/all_to_all | solution.py:60
  18.9 0.0 all-gather.3.cloned.1.call-start
  19.0 0.0 copy-start.4
  19.0 15.4 %all-to-all-done = bf16[8,32,2048]{2,1,0:T(8,128)(2,1)} async-done(((bf16[8,32,2048]{2,1,0:T(8,128)(2,1)}), bf16[8,32,2048]{2,1,0:T(8,128)(2,1)}, u32[]{:S(2)}, u32[]{:S(2)}) %all-to-all-start) | async-done | bytes 1048608 | tf_op jit(solution)/shard_map/all_to_all | solution.py:60
  34.4 2.4 %fusion.24 = bf16[128,2048]{1,0:T(8,128)(2,1)} fusion(bf16[8,32,2048]{2,1,0:T(8,128)(2,1)} %all-to-all-done, pred[128,32]{0,1:T(8,128)(4,1)S(1)} %iota_compare_fusion.4, pred[128,8]{0,1:T(8,128)(4,1)S(1)} %iota_compare_fusion.5), kind=kOutput, calls=%fused_computation.20 | convolution fusion | flops 134512640 | bytes 1577984 | tf_op jit(solution)/shard_map/csm,smd->cd/dot_general | solution.py:61
  36.7 0.0 copy-done.5
  36.7 0.0 all-gather.3.cloned.1.call-update
  36.8 0.0 reduce-scatter.2.cloned.1.call-start
  36.8 45.6 %all-gather.3.cloned.1.call-done = bf16[512,2048]{1,0:T(8,128)(2,1)} async-done(((bf16[128,2048]{1,0:T(8,128)(2,1)}), bf16[512,2048]{1,0:T(8,128)(2,1)}) %all-gather.3.cloned.1.call-update) | async-done | bytes 2097168 | tf_op jit(solution)/shard_map/all_gather | solution.py:67
  82.4 7.8 %fusion.21 = f32[512,1280]{1,0:T(8,128)} fusion(bf16[512,2048]{1,0:T(8,128)(2,1)} %all-gather.3.cloned.1.call-done, bf16[1,2048,1280]{2,1,0:T(8,128)(2,1)} %param.12), kind=kOutput, calls=%fused_computation.16 | convolution fusion | flops 2689597440 | bytes 9961472 | tf_op jit(solution)/shard_map/dot_general | solution.py:68
  90.2 0.0 copy-done.4
  90.2 13.1 %fusion.12 = bf16[512,2048]{1,0:T(8,128)(2,1)} fusion(bf16[1,1280,2048]{2,1,0:T(8,128)(2,1)} %param.14, f32[512,1280]{1,0:T(8,128)} %fusion.21, bf16[512,2048]{1,0:T(8,128)(2,1)} %all-gather.3.cloned.1.call-done, bf16[1,2048,1280]{2,1,0:T(8,128)(2,1)} %param.13), kind=kOutput, calls=%fused_computation.9 | convolution fusion | flops 5371068416 | bytes 17301504 | tf_op jit(solution)/shard_map/dot_general | solution.py:72
  103.3 0.0 copy-start.3
  103.3 0.0 copy-start.1
  103.3 0.0 reduce-scatter.2.cloned.1.call-update
  103.4 42.6 %reduce-scatter.2.cloned.1.call-done = bf16[128,2048]{1,0:T(8,128)(2,1)} async-done(((bf16[512,2048]{1,0:T(8,128)(2,1)}), bf16[128,2048]{1,0:T(8,128)(2,1)}) %reduce-scatter.2.cloned.1.call-update) | async-done | bytes 524304 | tf_op jit(solution)/shard_map/reduce_scatter | solution.py:71
  145.9 2.5 %convolution_convert_fusion = bf16[8,32,2048]{2,1,0:T(8,128)(2,1)} fusion(bf16[128,2048]{1,0:T(8,128)(2,1)} %reduce-scatter.2.cloned.1.call-done, pred[128,32]{0,1:T(8,128)(4,1)S(1)} %iota_compare_fusion.4, pred[128,8]{0,1:T(8,128)(4,1)} %copy-done.4), kind=kOutput, calls=%fused_computation.17 | convolution fusion | flops 134774784 | bytes 1577984 | tf_op jit(solution)/shard_map/csm,cd->smd/dot_general | solution.py:77
  148.4 4.2 %all-to-all-start.1 = ((bf16[8,32,2048]{2,1,0:T(8,128)(2,1)}), bf16[8,32,2048]{2,1,0:T(8,128)(2,1)}, u32[]{:S(2)}, u32[]{:S(2)}) async-start(bf16[8,32,2048]{2,1,0:T(8,128)(2,1)} %convolution_convert_fusion), calls=%async_computation.2 | async-start | bytes 2097152 | tf_op jit(solution)/shard_map/all_to_all | solution.py:80
  152.7 0.2 all-gather.5.cloned.1.call-start
  152.9 0.0 copy-done.3
  152.9 0.6 convert_element_type.61
  153.5 0.0 copy-done.1
  153.5 1.0 fusion.29
  154.5 13.5 %all-to-all-done.1 = bf16[8,32,2048]{2,1,0:T(8,128)(2,1)} async-done(((bf16[8,32,2048]{2,1,0:T(8,128)(2,1)}), bf16[8,32,2048]{2,1,0:T(8,128)(2,1)}, u32[]{:S(2)}, u32[]{:S(2)}) %all-to-all-start.1) | async-done | bytes 1048608 | tf_op jit(solution)/shard_map/all_to_all | solution.py:80
  168.0 2.0 fusion.32
  170.1 0.0 copy-start.2
  170.1 0.7 copy-done.2
  170.8 1.5 fusion.34
  172.3 0.0 all-gather.5.cloned.1.call-update
  172.4 25.5 %all-gather.5.cloned.1.call-done = bf16[512,2048]{1,0:T(8,128)(2,1)} async-done(((bf16[64,2048]{1,0:T(8,128)(2,1)}), bf16[512,2048]{1,0:T(8,128)(2,1)}) %all-gather.5.cloned.1.call-update) | async-done | bytes 2097168 | tf_op jit(solution)/shard_map/all_gather | solution.py:89
  197.9 0.0 copy-done
  197.9 4.3 %convolution_convert_fusion.2 = bf16[512,768]{1,0:T(8,128)(2,1)} fusion(bf16[512,2048]{1,0:T(8,128)(2,1)} %all-gather.5.cloned.1.call-done, bf16[2048,768]{0,1:T(8,128)(2,1)S(1)} %bitcast.80), kind=kOutput, calls=%fused_computation.24 | convolution fusion | flops 1611005952 | bytes 6029312 | tf_op jit(solution)/shard_map/dot_general | solution.py:88
  202.2 2.3 %copy.13 = bf16[512,768]{0,1:T(8,128)(2,1)} copy(bf16[512,768]{1,0:T(8,128)(2,1)} %convolution_convert_fusion.2) | data formatting | bytes 1572864 | tf_op jit(solution)/shard_map/convert_element_type | solution.py:92
  (6 shorter events, 0.1 us)
Async XLA Ops:
  7.2 190.7 %copy-start = (bf16[2048,1,6,2,64]{0,4,3,2,1:T(8,128)(2,1)S(1)}, bf16[2048,1,6,2,64]{0,4,3,2,1:T(8,128)(2,1)}, u32[]{:S(2)}) copy-start(bf16[2048,1,6,2,64]{0,4,3,2,1:T(8,128)(2,1)} %param.17) | copy-start | bytes 9437188
  10.6 26.1 %copy-start.5 = (f32[64]{0:T(128)}, f32[64]{0:T(128)S(1)}, u32[]{:S(2)}) copy-start(f32[64]{0:T(128)S(1)} %add_rsqrt_fusion.1) | copy-start | bytes 772
  13.7 20.7 %all-to-all-start = ((bf16[8,32,2048]{2,1,0:T(8,128)(2,1)}), bf16[8,32,2048]{2,1,0:T(8,128)(2,1)}, u32[]{:S(2)}, u32[]{:S(2)}) async-start(bf16[8,32,2048]{2,1,0:T(8,128)(2,1)} %convolution_convert_fusion.1), calls=%async_computation | async-start | bytes 2097152 | tf_op jit(solution)/shard_map/all_to_all | solution.py:60
  18.9 63.5 %all-gather.3.cloned.1.call-start = ((), (), s32[]{:S(2)}) async-start(), calls=%async_computation.3 | async-start | bytes 2621440 | tf_op jit(solution)/shard_map/all_gather | solution.py:67
  19.0 71.3 %copy-start.4 = (pred[128,8]{0,1:T(8,128)(4,1)}, pred[128,8]{0,1:T(8,128)(4,1)S(1)}, u32[]{:S(2)}) copy-start(pred[128,8]{0,1:T(8,128)(4,1)S(1)} %iota_compare_fusion.5) | copy-start | bytes 3076
  36.8 109.2 %reduce-scatter.2.cloned.1.call-start = ((), (), s32[]{:S(2)}) async-start(), calls=%async_computation.4 | async-start | bytes 2621440 | tf_op jit(solution)/shard_map/reduce_scatter | solution.py:71
  103.3 49.6 %copy-start.3 = (bf16[2048]{0:T(1024)(128)(2,1)S(1)}, bf16[2048]{0:T(1024)(128)(2,1)}, u32[]{:S(2)}) copy-start(bf16[2048]{0:T(1024)(128)(2,1)} %param.16) | copy-start | bytes 12292
  103.3 50.2 %copy-start.1 = (bf16[64,2048]{1,0:T(8,128)(2,1)S(1)}, bf16[64,2048]{1,0:T(8,128)(2,1)}, u32[]{:S(2)}) copy-start(bf16[64,2048]{1,0:T(8,128)(2,1)} %param.9) | copy-start | bytes 786436
  148.4 19.6 %all-to-all-start.1 = ((bf16[8,32,2048]{2,1,0:T(8,128)(2,1)}), bf16[8,32,2048]{2,1,0:T(8,128)(2,1)}, u32[]{:S(2)}, u32[]{:S(2)}) async-start(bf16[8,32,2048]{2,1,0:T(8,128)(2,1)} %convolution_convert_fusion), calls=%async_computation.2 | async-start | bytes 2097152 | tf_op jit(solution)/shard_map/all_to_all | solution.py:80
  152.7 45.2 %all-gather.5.cloned.1.call-start = ((), (), s32[]{:S(2)}) async-start(), calls=%async_computation.5 | async-start | bytes 2359296 | tf_op jit(solution)/shard_map/all_gather | solution.py:89
  170.1 0.7 copy-start.2
Sparse Core Ops, SparseCore 0:
  36.9 45.4 all-gather.2
  103.5 42.4 reduce-scatter.1
  172.5 25.3 all-gather.4
where the time goes:
time: 212 us; the launch traced here: 211 us
  waiting for transfers between devices  143 us (67%)
  matrix products  35.8 us (17%)
  between operations  13.9 us (7%)
  starting transfers between devices  9.75 us (5%)
  other arithmetic  5.95 us (3%)
  local copies, waits for them, and re-layouts  3.02 us (1%)
    all_gather x1, waiting for transfers between devices, local(): block_rows = lax.all_gather(picked, 'dp', axis=0, tiled=True)  45.6 us
    reduce_scatter x1, waiting for transfers between devices, local(): lax.psum_scatter(jnp.dot(hidden_all, down_proj, preferred_element_type=jn...  42.6 us
    all_gather x1, waiting for transfers between devices, local(): lax.all_gather(encoded, 'expert', axis=0, tiled=True)  25.5 us
    all_to_all x1, waiting for transfers between devices, local(): lax.all_to_all(outgoing, 'expert', split_axis=0, concat_axis=0, tiled=True)  15.4 us
    all_to_all x1, waiting for transfers between devices, local(): lax.all_to_all(outbound, 'expert', split_axis=0, concat_axis=0, tiled=True)  13.5 us
    dot_general x1, matrix products, local(): jnp.dot(hidden_all, down_proj, preferred_element_type=jnp.float32)  13.1 us
    dot_general x1, matrix products, local(): jnp.dot(block_rows, gate_proj, preferred_element_type=jnp.float32)  7.82 us
    all_to_all x1, starting transfers between devices, local(): lax.all_to_all(outgoing, 'expert', split_axis=0, concat_axis=0, tiled=True)  5.2 us
  transfers between devices with their start and end apart: 5, of which 5 were waited for; matrix products, arithmetic and copies ran while one was open for 1% of the time, Pallas kernels for 0%

commit v1 on v0

v1 whole, which is shorter than its diff:
```python
import functools

import jax
import jax.numpy as jnp
from jax import lax
from jax.experimental import pallas as pl
from jax.experimental.pallas import tpu as pltpu
from jax.sharding import PartitionSpec as P

MESH = pl.DeviceIdType.MESH


def normalize(values, gain):
    return (
        values
        * lax.rsqrt(jnp.mean(values * values, axis=-1, keepdims=True) + 1e-06)
        * gain.astype(jnp.float32)
    )


def kernel(
    n, experts, chunks,
    normed, tokens, pick_map, out_map, weight_hi, weight_lo, gain, gate_hbm, up_hbm, down_hbm,
    moe_out, encoded_all,
    gate_w, up_w, down_w, normed_all, gathered, hidden, part, sums, summed, outbound, returned, encoded,
    load_sem, ag_send, ag_recv, z_send, z_recv, rs_send, rs_recv, back_send, back_recv, enc_send, enc_recv,
):
    p = lax.axis_index("dp")
    me = lax.axis_index("expert")
    rows, width = normed.shape
    cap = pick_map.shape[0]
    slots = outbound.shape[1]
    ff = gate_w.shape[1]
    chips = experts // 2
    core = lax.rem(me, 2)
    chip = lax.div(me, 2)
    partner = chip * 2 + (1 - core)
    ch_rows = cap // chunks

    loads = [
        pltpu.make_async_copy(src.at[0], dst, load_sem.at[i])
        for i, (src, dst) in enumerate(((gate_hbm, gate_w), (up_hbm, up_w), (down_hbm, down_w)))
    ]
    for load in loads:
        load.start()

    barrier = pltpu.get_barrier_semaphore()

    @pl.loop(1, experts)
    def _(k):
        pl.semaphore_signal(barrier, inc=1, device_id={"expert": lax.rem(me + k, experts)}, device_id_type=MESH)

    @pl.when(p > 0)
    def _():
        pl.semaphore_signal(barrier, inc=1, device_id={"dp": p - 1}, device_id_type=MESH)

    @pl.when(p < n - 1)
    def _():
        pl.semaphore_signal(barrier, inc=1, device_id={"dp": p + 1}, device_id_type=MESH)

    neighbours = jnp.where(p > 0, 1, 0) + jnp.where(p < n - 1, 1, 0)
    pl.semaphore_wait(barrier, experts - 1 + neighbours)

    def span(index, size):
        return pl.ds(pl.multiple_of(index * size, size), size)

    def plane_gather(own, full, send, recv):
        def copy(source, src, target, slot):
            return pltpu.make_async_remote_copy(
                src_ref=src,
                dst_ref=full.at[span(source, rows)],
                send_sem=send.at[slot],
                recv_sem=recv.at[source],
                device_id={"expert": target},
                device_id_type=MESH,
            )

        @pl.loop(1, chips)
        def _(k):
            copy(me, own, lax.rem(chip + k, chips) * 2 + core, k).start()

        copy(me, own, partner, 0).start()
        full[span(me, rows)] = own[...]

        @pl.loop(1, chips)
        def _(k):
            source = lax.rem(chip + chips - k, chips) * 2 + core
            piece = copy(source, full.at[span(source, rows)], partner, chips + k)
            piece.wait_recv()
            piece.start()

        copy(partner, own, partner, 0).wait_recv()

        @pl.loop(1, chips)
        def _(k):
            copy(lax.rem(chip + chips - k, chips) * 2 + 1 - core, own, partner, 0).wait_recv()

        copy(me, own, partner, 0).wait_send()

        @pl.loop(1, chips)
        def _(k):
            copy(me, own, partner, k).wait_send()
            copy(me, own, partner, chips + k).wait_send()

    with jax.named_scope("gather_normed"):
        plane_gather(normed, normed_all, ag_send, ag_recv)

    tile = 512

    @pl.loop(0, width // tile)
    def _(i):
        cols = span(i, tile)
        gathered[p, :, cols] = jnp.dot(
            pick_map[...], normed_all[:, cols], preferred_element_type=jnp.float32
        ).astype(jnp.bfloat16)

    def z_copy(g, c, way, target):
        piece = gathered.at[g, span(c, ch_rows)]
        return pltpu.make_async_remote_copy(
            src_ref=piece,
            dst_ref=piece,
            send_sem=z_send.at[way, g, c],
            recv_sem=z_recv.at[g, c],
            device_id={"dp": target},
            device_id_type=MESH,
        )

    def rs_copy(g, c, slot, target):
        return pltpu.make_async_remote_copy(
            src_ref=part.at[g, span(c, ch_rows)],
            dst_ref=sums.at[slot, span(c, ch_rows)],
            send_sem=rs_send.at[g, c],
            recv_sem=rs_recv.at[slot, c],
            device_id={"dp": target},
            device_id_type=MESH,
        )

    def rs_start(g, c):
        @pl.when(g < p)
        def _():
            rs_copy(g, c, g, p - 1).start()

        @pl.when(g > p)
        def _():
            rs_copy(g, c, jnp.where(g == p + 1, n, g), p + 1).start()

    @pl.loop(0, chunks)
    def _(c):
        @pl.when(p < n - 1)
        def _():
            z_copy(p, c, 0, p + 1).start()

        @pl.when(p > 0)
        def _():
            z_copy(p, c, 1, p - 1).start()

    for load in loads:
        load.wait()

    ff_tile = 256 if ff % 256 == 0 else 128

    @pl.loop(0, 2 * n - 1)
    def _(j):
        k = lax.div(j + 1, 2)
        odd = lax.rem(j, 2)
        g = p + k * (1 - 2 * odd)

        @pl.when((g >= 0) & (g < n))
        def _():
            @pl.loop(0, chunks)
            def _(c):
                @pl.when(g != p)
                def _():
                    z_copy(g, c, 0, p).wait_recv()

                @pl.when((g < p) & (p < n - 1))
                def _():
                    z_copy(g, c, 0, p + 1).start()

                @pl.when((g > p) & (p > 0))
                def _():
                    z_copy(g, c, 1, p - 1).start()

            @pl.loop(0, ff // ff_tile)
            def _(i):
                cols = span(i, ff_tile)
                block = gathered[g]
                gate = jnp.dot(block, gate_w[:, cols], preferred_element_type=jnp.float32)
                up = jnp.dot(block, up_w[:, cols], preferred_element_type=jnp.float32)
                hidden[:, cols] = (jax.nn.gelu(gate, approximate=True) * up).astype(jnp.bfloat16)

            @pl.loop(0, width // tile)
            def _(i):
                cols = span(i, tile)
                part[g, :, cols] = jnp.dot(
                    hidden[...], down_w[:, cols], preferred_element_type=jnp.float32
                ).astype(jnp.bfloat16)

            @pl.when(((g < p) & (p == n - 1)) | ((g > p) & (p == 0)))
            def _():
                @pl.loop(0, chunks)
                def _(c):
                    rs_start(g, c)

    left_first = jnp.where(2 * p >= n - 1, 1, 0)

    @pl.loop(0, 2 * (n - 1))
    def _(j):
        is_left = jnp.where(j < n - 1, left_first, 1 - left_first)
        g = p + (1 + lax.rem(j, n - 1)) * (1 - 2 * is_left)
        inner = jnp.where(is_left == 1, (g >= 0) & (p < n - 1), (g < n) & (p > 0))

        @pl.when(inner)
        def _():
            @pl.loop(0, chunks)
            def _(c):
                piece = span(c, ch_rows)
                rs_copy(g, c, g, p).wait_recv()
                part[g, piece] = (
                    part[g, piece].astype(jnp.float32) + sums[g, piece].astype(jnp.float32)
                ).astype(jnp.bfloat16)
                rs_start(g, c)

    @pl.loop(0, chunks)
    def _(c):
        piece = span(c, ch_rows)

        @pl.when(p < n - 1)
        def _():
            rs_copy(p, c, p, p).wait_recv()

        @pl.when(p > 0)
        def _():
            rs_copy(p, c, n, p).wait_recv()

        @pl.when((p > 0) & (p < n - 1))
        def _():
            summed[piece] = (
                part[p, piece].astype(jnp.float32)
                + sums[p, piece].astype(jnp.float32)
                + sums[n, piece].astype(jnp.float32)
            ).astype(jnp.bfloat16)

        @pl.when((p > 0) & (p == n - 1))
        def _():
            summed[piece] = (
                part[p, piece].astype(jnp.float32) + sums[n, piece].astype(jnp.float32)
            ).astype(jnp.bfloat16)

        @pl.when((p == 0) & (p < n - 1))
        def _():
            summed[piece] = (
                part[p, piece].astype(jnp.float32) + sums[p, piece].astype(jnp.float32)
            ).astype(jnp.bfloat16)

    def back_copy(source, target):
        return pltpu.make_async_remote_copy(
            src_ref=outbound.at[target],
            dst_ref=returned.at[span(source, slots)],
            send_sem=back_send.at[target],
            recv_sem=back_recv.at[source],
            device_id={"expert": target},
            device_id_type=MESH,
        )

    @pl.loop(1, experts + 1)
    def _(k):
        target = lax.rem(me + k, experts)
        outbound[target] = jnp.dot(
            out_map[span(target, slots)], summed[...], preferred_element_type=jnp.float32
        ).astype(jnp.bfloat16)

        @pl.when(k < experts)
        def _():
            back_copy(me, target).start()

    returned[span(me, slots)] = outbound[me]

    @pl.loop(1, experts)
    def _(k):
        back_copy(lax.rem(me + k, experts), me).wait_recv()

    square = jnp.zeros((rows, 1), jnp.float32)
    for i in range(width // tile):
        cols = pl.ds(i * tile, tile)
        block = returned[:, cols]
        value = (
            tokens[:, cols].astype(jnp.float32)
            + jnp.dot(weight_hi[...], block, preferred_element_type=jnp.float32)
            + jnp.dot(weight_lo[...], block, preferred_element_type=jnp.float32)
        ).astype(jnp.bfloat16)
        moe_out[:, cols] = value
        wide = value.astype(jnp.float32)
        square = square + jnp.sum(wide * wide, axis=1, keepdims=True)
    scale = lax.rsqrt(square / width + 1e-06)
    for i in range(width // tile):
        cols = pl.ds(i * tile, tile)
        encoded[:, cols] = (
            moe_out[:, cols].astype(jnp.float32) * scale * gain[:, cols].astype(jnp.float32)
        ).astype(jnp.bfloat16)

    with jax.named_scope("gather_encoded"):
        plane_gather(encoded, encoded_all, enc_send, enc_recv)

    @pl.loop(1, experts)
    def _(k):
        back_copy(me, lax.rem(me + k, experts)).wait_send()

    @pl.loop(0, n)
    def _(g):
        @pl.loop(0, chunks)
        def _(c):
            @pl.when((g <= p) & (p < n - 1))
            def _():
                z_copy(g, c, 0, p).wait_send()

            @pl.when((g >= p) & (p > 0))
            def _():
                z_copy(g, c, 1, p).wait_send()

            @pl.when(g != p)
            def _():
                rs_copy(g, c, g, p).wait_send()


def local(
    tokens,
    norm_gain,
    router_weight,
    gate_weight,
    up_weight,
    down_weight,
    expert_picks,
    final_gain,
    kv_weight,
):
    n = lax.axis_size("dp")
    experts = lax.axis_size("expert")
    me = lax.axis_index("expert")
    rows, width = tokens.shape
    ff = gate_weight.shape[2]
    chosen = expert_picks[0]
    cap = chosen.shape[1]
    slots = 4 * rows // experts
    wide_tokens = tokens.astype(jnp.float32)
    normed = normalize(wide_tokens, norm_gain).astype(jnp.bfloat16)
    gate_probs = jax.nn.sigmoid(jnp.dot(normed, router_weight, preferred_element_type=jnp.float32))
    source = chosen // rows
    local_row = chosen % rows
    positions = jnp.arange(cap, dtype=jnp.int32)
    earlier = (source[:, :, None] == source[:, None, :]) & (
        positions[None, None, :] < positions[None, :, None]
    )
    slot_rank = jnp.sum(earlier.astype(jnp.int32), axis=2)
    own_chosen = lax.dynamic_index_in_dim(chosen, me, 0, keepdims=False)
    own_rank = lax.dynamic_index_in_dim(slot_rank, me, 0, keepdims=False)
    own_slot = (own_chosen // rows) * slots + own_rank
    pick_map = (own_chosen[:, None] == jnp.arange(experts * rows, dtype=jnp.int32)[None, :]).astype(jnp.bfloat16)
    out_map = (jnp.arange(experts * slots, dtype=jnp.int32)[:, None] == own_slot[None, :]).astype(jnp.bfloat16)
    send_slot = (
        (source == me)[:, :, None] & (slot_rank[:, :, None] == jnp.arange(slots, dtype=jnp.int32))
    ).astype(jnp.bfloat16)
    local_map = (local_row[:, :, None] == jnp.arange(rows, dtype=jnp.int32)).astype(jnp.bfloat16)
    send_map = jnp.einsum("ecm,ect->tem", send_slot, local_map, preferred_element_type=jnp.float32)
    weight = (send_map * gate_probs[:, :, None]).reshape(rows, experts * slots)
    weight_hi = lax.reduce_precision(weight, 8, 7)
    weight_lo = (weight - weight_hi).astype(jnp.bfloat16)
    weight_hi = weight_hi.astype(jnp.bfloat16)

    chunks = 4
    bf16 = jnp.bfloat16
    dma = pltpu.SemaphoreType.DMA
    vmem = pl.BlockSpec(memory_space=pltpu.VMEM)
    hbm = pl.BlockSpec(memory_space=pl.ANY)
    moe_out, encoded_all = pl.pallas_call(
        functools.partial(kernel, n, experts, chunks),
        out_shape=(
            jax.ShapeDtypeStruct((rows, width), bf16),
            jax.ShapeDtypeStruct((experts * rows, width), bf16),
        ),
        in_specs=[vmem] * 7 + [hbm] * 3,
        out_specs=(vmem, vmem),
        scratch_shapes=[
            pltpu.VMEM((width, ff), bf16),
            pltpu.VMEM((width, ff), bf16),
            pltpu.VMEM((ff, width), bf16),
            pltpu.VMEM((experts * rows, width), bf16),
            pltpu.VMEM((n, cap, width), bf16),
            pltpu.VMEM((cap, ff), bf16),
            pltpu.VMEM((n, cap, width), bf16),
            pltpu.VMEM((n + 1, cap, width), bf16),
            pltpu.VMEM((cap, width), bf16),
            pltpu.VMEM((experts, slots, width), bf16),
            pltpu.VMEM((experts * slots, width), bf16),
            pltpu.VMEM((rows, width), bf16),
            dma((3,)),
            dma((experts,)),
            dma((experts,)),
            dma((2, n, chunks)),
            dma((n, chunks)),
            dma((n, chunks)),
            dma((n + 1, chunks)),
            dma((experts,)),
            dma((experts,)),
            dma((experts,)),
            dma((experts,)),
        ],
        compiler_params=pltpu.CompilerParams(
            collective_id=0, has_side_effects=True, vmem_limit_bytes=60 * 1024 * 1024
        ),
    )(
        normed, tokens, pick_map, out_map, weight_hi, weight_lo, final_gain[None, :],
        gate_weight, up_weight, down_weight,
    )
    kv_matrix = kv_weight.reshape(kv_weight.shape[0], -1)
    kv_rows = lax.dot_general(
        kv_matrix, encoded_all, (((0,), (1,)), ((), ())), preferred_element_type=jnp.float32
    ).astype(jnp.bfloat16)
    kv_cache = kv_rows.T.reshape((encoded_all.shape[0],) + kv_weight.shape[1:])
    return (moe_out, kv_cache)


def solution(mesh):
    in_specs = (
        P(("dp", "expert"), None),
        P(),
        P(),
        P("expert", None, "dp"),
        P("expert", None, "dp"),
        P("expert", "dp", None),
        P("dp", None, None),
        P(),
        P(None, "expert", None, None, None),
    )
    out_specs = (P(("dp", "expert"), None), P("dp", "expert", None, None, None))
    return jax.shard_map(local, mesh=mesh, in_specs=in_specs, out_specs=out_specs, check_vma=False)
```

time: 212 us -> 142 us (0.67)
  waiting for transfers between devices: 143 us -> 0 us
  Pallas kernels: 0 us -> 119 us
  matrix products: 35.8 us -> 6.22 us
  between operations: 13.9 us -> 0.7 us
  starting transfers between devices: 9.75 us -> 0 us
  local copies, waits for them, and re-layouts: 3.02 us -> 7.86 us
    pallas_call x0 -> x1, Pallas kernels: none -> 119 us  [local(): pl.pallas_call(functools.partial(kernel, n, experts, chunks), out_shape=(...]
    all_gather x2 -> x0, waiting for transfers between devices: 71.1 us -> none  [the longest x1 45.6 us: local(): block_rows = lax.all_gather(picked, 'dp', axis=0, tiled=True)]
    reduce_scatter x1 -> x0, waiting for transfers between devices: 42.6 us -> none  [local(): lax.psum_scatter(jnp.dot(hidden_all, down_proj, preferred_element_type=jn...]
    dot_general x8 -> x2, matrix products: 34.8 us -> 5.26 us  [the longest x1 4.4 us: local(): lax.dot_general(kv_matrix, encoded_all, (((0,), (1,)), ((), ())), preferr...]
    all_to_all x2 -> x0, waiting for transfers between devices: 28.9 us -> none  [the longest x1 15.4 us: local(): lax.all_to_all(outgoing, 'expert', split_axis=0, concat_axis=0, tiled=True)]
    all_to_all x2 -> x0, starting transfers between devices: 9.45 us -> none  [the longest x1 5.2 us: local(): lax.all_to_all(outgoing, 'expert', split_axis=0, concat_axis=0, tiled=True)]
  transfers between devices with their start and end apart: 5 -> 0, of which waited for: 5 -> 0; matrix products, arithmetic and copies ran while one was open for 1% -> 0% of each run, Pallas kernels for 0% -> 0%
where the time goes in v1:
time: 142 us; the launch traced here: 141 us
  Pallas kernels  119 us (84%)
  local copies, waits for them, and re-layouts  7.86 us (6%)
  other arithmetic  7.4 us (5%)
  matrix products  6.22 us (4%)
    pallas_call x1, Pallas kernels, local(): pl.pallas_call(functools.partial(kernel, n, experts, chunks), out_shape=(...  119 us
    dot_general x1, matrix products, local(): lax.dot_general(kv_matrix, encoded_all, (((0,), (1,)), ((), ())), preferr...  4.4 us

profile of v1, /device:TPU:0, one launch (start us, length us, event | category | flops | bytes accessed | tf_op | source)
XLA Modules:
  0.0 141.2 jit_solution(15021157223550016142)
XLA Ops:
  0.6 0.0 copy-start
  0.6 1.9 %copy-done = bf16[2048,1,6,2,64]{0,4,3,2,1:T(8,128)(2,1)S(1)} copy-done((bf16[2048,1,6,2,64]{0,4,3,2,1:T(8,128)(2,1)S(1)}, bf16[2048,1,6,2,64]{0,4,3,2,1:T(8,128)(2,1)}, u32[]{:S(2)}) %copy-start) | copy-done | bytes 3145752
  2.5 1.1 fusion.4
  3.6 0.7 fusion.18
  4.3 0.7 add_select_fusion
  5.0 0.7 broadcast_compare_fusion
  5.7 0.7 convert_element_type.31
  6.4 1.3 broadcast_in_dim.2.gain
  7.7 0.4 convert_reduce_fusion
  8.1 0.7 add_bitcast_fusion
  8.8 0.7 fusion.9.out_map
  9.5 0.7 fusion.7.pick_map
  10.2 1.1 fusion.6.normed
  11.3 0.0 copy-start.1
  11.3 1.0 fusion.3
  12.3 0.9 fusion
  13.1 1.0 copy.16
  14.1 0.6 fusion.12
  14.8 0.0 copy-done.1
  14.8 119.0 %shard_map.104 = (bf16[64,2048]{1,0:T(8,128)(2,1)}, bf16[512,2048]{1,0:T(8,128)(2,1)}) custom-call(bf16[64,2048]{1,0:T(8,128)(2,1)} %copy-done.1, bf16[64,2048]{1,0:T(8,128)(2,1)} %tokens.1, bf16[128,512]{1,0:T(8,128)(2,1)} %fusion.7.pick_map, bf16[256,128]{1,0:T(8,128)(2,1)} %fusion.9.out_map, bf16[64,256]{1,0:T(8,128)(2,1)} %get-tuple-element.11.weight_hi, ...), custom_call_target="tpu_custom_call" | custom-call | tf_op jit(solution)/shard_map/pallas_call | solution.py:375
  133.8 0.0 copy-start.2
  133.8 4.4 %convolution_convert_fusion = bf16[512,768]{1,0:T(8,128)(2,1)} fusion(bf16[512,2048]{1,0:T(8,128)(2,1)} %get-tuple-element.5, bf16[2048,768]{0,1:T(8,128)(2,1)S(1)} %bitcast.52), kind=kOutput, calls=%fused_computation | convolution fusion | flops 1611005952 | bytes 6029312 | tf_op jit(solution)/shard_map/dot_general | solution.py:416
  138.2 2.3 %copy.18 = bf16[512,768]{0,1:T(8,128)(2,1)} copy(bf16[512,768]{1,0:T(8,128)(2,1)} %convolution_convert_fusion) | data formatting | bytes 1572864 | tf_op jit(solution)/shard_map/convert_element_type | solution.py:418
  140.5 0.0 copy-done.2
  140.5 0.7 copy.20
  (2 shorter events, 0.0 us)
Async XLA Ops:
  0.6 1.9 %copy-start = (bf16[2048,1,6,2,64]{0,4,3,2,1:T(8,128)(2,1)S(1)}, bf16[2048,1,6,2,64]{0,4,3,2,1:T(8,128)(2,1)}, u32[]{:S(2)}) copy-start(bf16[2048,1,6,2,64]{0,4,3,2,1:T(8,128)(2,1)} %param.17) | copy-start | bytes 9437188
  11.3 3.5 %copy-start.1 = (bf16[64,2048]{1,0:T(8,128)(2,1)}, bf16[64,2048]{1,0:T(8,128)(2,1)S(1)}, u32[]{:S(2)}) copy-start(bf16[64,2048]{1,0:T(8,128)(2,1)S(1)} %fusion.6.normed) | copy-start | bytes 786436
  133.8 6.7 %copy-start.2 = (bf16[64,2048]{1,0:T(8,128)(2,1)S(1)}, bf16[64,2048]{1,0:T(8,128)(2,1)}, u32[]{:S(2)}) copy-start(bf16[64,2048]{1,0:T(8,128)(2,1)} %get-tuple-element.14) | copy-start | bytes 786436

commit v2 on v1

v2 whole, which is shorter than its diff:
```python
import functools

import jax
import jax.numpy as jnp
from jax import lax
from jax.experimental import pallas as pl
from jax.experimental.pallas import tpu as pltpu
from jax.sharding import PartitionSpec as P

MESH = pl.DeviceIdType.MESH


def normalize(values, gain):
    return (
        values
        * lax.rsqrt(jnp.mean(values * values, axis=-1, keepdims=True) + 1e-06)
        * gain.astype(jnp.float32)
    )


def kernel(
    n, experts, chunks,
    normed, tokens, pick_map, out_map, weight_hi, weight_lo, gate_hbm, up_hbm, down_hbm,
    moe_out, encoded_all,
    gate_w, up_w, down_w, normed_all, gathered, hidden, part, sums, outbound, returned, encoded,
    load_sem, ag_send, ag_recv, z_send, z_recv, rs_send, rs_recv, back_send, back_recv, enc_send, enc_recv,
):
    p = lax.axis_index("dp")
    me = lax.axis_index("expert")
    rows, width = normed.shape
    cap = pick_map.shape[0]
    slots = outbound.shape[0] // experts
    ff = gate_w.shape[1]
    chips = experts // 2
    core = lax.rem(me, 2)
    chip = lax.div(me, 2)
    partner = chip * 2 + (1 - core)

    loads = [
        pltpu.make_async_copy(src.at[0], dst, load_sem.at[i])
        for i, (src, dst) in enumerate(((gate_hbm, gate_w), (up_hbm, up_w), (down_hbm, down_w)))
    ]
    for load in loads:
        load.start()

    barrier = pltpu.get_barrier_semaphore()

    @pl.loop(1, experts)
    def _(k):
        pl.semaphore_signal(barrier, inc=1, device_id={"expert": lax.rem(me + k, experts)}, device_id_type=MESH)

    @pl.when(p > 0)
    def _():
        pl.semaphore_signal(barrier, inc=1, device_id={"dp": p - 1}, device_id_type=MESH)

    @pl.when(p < n - 1)
    def _():
        pl.semaphore_signal(barrier, inc=1, device_id={"dp": p + 1}, device_id_type=MESH)

    neighbours = jnp.where(p > 0, 1, 0) + jnp.where(p < n - 1, 1, 0)
    pl.semaphore_wait(barrier, experts - 1 + neighbours)

    def span(index, size):
        return pl.ds(pl.multiple_of(index * size, size), size)

    tile = width // chunks

    def plane_copy(own, full, send, recv, c, source, target, slot, relay=False):
        cols = span(c, tile)
        place = full.at[span(source, rows), cols]
        return pltpu.make_async_remote_copy(
            src_ref=place if relay else own.at[:, cols],
            dst_ref=place,
            send_sem=send.at[slot, c],
            recv_sem=recv.at[source, c],
            device_id={"expert": target},
            device_id_type=MESH,
        )

    def plane_start(args, c):
        @pl.loop(1, chips)
        def _(k):
            plane_copy(*args, c, me, lax.rem(chip + k, chips) * 2 + core, k).start()

        plane_copy(*args, c, me, partner, 0).start()

    def plane_relay(args, c):
        @pl.loop(1, chips)
        def _(k):
            source = lax.rem(chip + chips - k, chips) * 2 + core
            piece = plane_copy(*args, c, source, partner, chips + k, relay=True)
            piece.wait_recv()
            piece.start()

    def plane_arrive(args, c):
        @pl.loop(0, chips)
        def _(k):
            plane_copy(*args, c, lax.rem(chip + k, chips) * 2 + 1 - core, partner, 0).wait_recv()

    def plane_finish(args, c):
        @pl.loop(0, chips)
        def _(k):
            plane_copy(*args, c, me, partner, k).wait_send()

        @pl.loop(1, chips)
        def _(k):
            plane_copy(*args, c, me, partner, chips + k).wait_send()

    first = (normed, normed_all, ag_send, ag_recv)

    @pl.loop(0, chunks)
    def _(c):
        plane_start(first, c)

    normed_all[span(me, rows)] = normed[...]

    def z_copy(g, c, way, target):
        piece = gathered.at[g, :, span(c, tile)]
        return pltpu.make_async_remote_copy(
            src_ref=piece,
            dst_ref=piece,
            send_sem=z_send.at[way, g, c],
            recv_sem=z_recv.at[g, c],
            device_id={"dp": target},
            device_id_type=MESH,
        )

    def rs_copy(g, c, slot, target):
        return pltpu.make_async_remote_copy(
            src_ref=part.at[g, :, span(c, tile)],
            dst_ref=sums.at[slot, :, span(c, tile)],
            send_sem=rs_send.at[g, c],
            recv_sem=rs_recv.at[slot, c],
            device_id={"dp": target},
            device_id_type=MESH,
        )

    def rs_start(g, c):
        @pl.when(g < p)
        def _():
            rs_copy(g, c, g, p - 1).start()

        @pl.when(g > p)
        def _():
            rs_copy(g, c, jnp.where(g == p + 1, n, g), p + 1).start()

    @pl.loop(0, chunks)
    def _(c):
        plane_relay(first, c)
        plane_arrive(first, c)
        gathered[p, :, span(c, tile)] = jnp.dot(
            pick_map[...], normed_all[:, span(c, tile)], preferred_element_type=jnp.float32
        ).astype(jnp.bfloat16)

        @pl.when(p < n - 1)
        def _():
            z_copy(p, c, 0, p + 1).start()

        @pl.when(p > 0)
        def _():
            z_copy(p, c, 1, p - 1).start()

    for load in loads:
        load.wait()

    ff_tile = 256 if ff % 256 == 0 else 128

    @pl.loop(0, 2 * n - 1)
    def _(j):
        k = lax.div(j + 1, 2)
        odd = lax.rem(j, 2)
        g = p + k * (1 - 2 * odd)

        @pl.when((g >= 0) & (g < n))
        def _():
            @pl.loop(0, chunks)
            def _(c):
                @pl.when(g != p)
                def _():
                    z_copy(g, c, 0, p).wait_recv()

                @pl.when((g < p) & (p < n - 1))
                def _():
                    z_copy(g, c, 0, p + 1).start()

                @pl.when((g > p) & (p > 0))
                def _():
                    z_copy(g, c, 1, p - 1).start()

            @pl.loop(0, ff // ff_tile)
            def _(i):
                cols = span(i, ff_tile)
                block = gathered[g]
                gate = jnp.dot(block, gate_w[:, cols], preferred_element_type=jnp.float32)
                up = jnp.dot(block, up_w[:, cols], preferred_element_type=jnp.float32)
                hidden[:, cols] = (jax.nn.gelu(gate, approximate=True) * up).astype(jnp.bfloat16)

            @pl.loop(0, chunks)
            def _(c):
                cols = span(c, tile)
                part[g, :, cols] = jnp.dot(
                    hidden[...], down_w[:, cols], preferred_element_type=jnp.float32
                ).astype(jnp.bfloat16)

                @pl.when(((g < p) & (p == n - 1)) | ((g > p) & (p == 0)))
                def _():
                    rs_start(g, c)

    left_first = jnp.where(2 * p >= n - 1, 1, 0)

    @pl.loop(0, 2 * (n - 1))
    def _(j):
        is_left = jnp.where(j < n - 1, left_first, 1 - left_first)
        g = p + (1 + lax.rem(j, n - 1)) * (1 - 2 * is_left)
        inner = jnp.where(is_left == 1, (g >= 0) & (p < n - 1), (g < n) & (p > 0))

        @pl.when(inner)
        def _():
            @pl.loop(0, chunks)
            def _(c):
                piece = span(c, tile)
                rs_copy(g, c, g, p).wait_recv()
                part[g, :, piece] = (
                    part[g, :, piece].astype(jnp.float32) + sums[g, :, piece].astype(jnp.float32)
                ).astype(jnp.bfloat16)
                rs_start(g, c)

    def back_copy(c, source, target):
        cols = span(c, tile)
        return pltpu.make_async_remote_copy(
            src_ref=outbound.at[span(target, slots), cols],
            dst_ref=returned.at[span(source, slots), cols],
            send_sem=back_send.at[target, c],
            recv_sem=back_recv.at[source, c],
            device_id={"expert": target},
            device_id_type=MESH,
        )

    second = (encoded, encoded_all, enc_send, enc_recv)

    @pl.loop(0, chunks + 2)
    def _(step):
        @pl.when(step < chunks)
        def _():
            c = step
            cols = span(c, tile)

            @pl.when(p < n - 1)
            def _():
                rs_copy(p, c, p, p).wait_recv()
                part[p, :, cols] = (
                    part[p, :, cols].astype(jnp.float32) + sums[p, :, cols].astype(jnp.float32)
                ).astype(jnp.bfloat16)

            @pl.when(p > 0)
            def _():
                rs_copy(p, c, n, p).wait_recv()
                part[p, :, cols] = (
                    part[p, :, cols].astype(jnp.float32) + sums[n, :, cols].astype(jnp.float32)
                ).astype(jnp.bfloat16)

            outbound[:, cols] = jnp.dot(
                out_map[...], part[p, :, cols], preferred_element_type=jnp.float32
            ).astype(jnp.bfloat16)

            @pl.loop(1, experts)
            def _(k):
                back_copy(c, me, lax.rem(me + k, experts)).start()

            returned[span(me, slots), cols] = outbound[span(me, slots), cols]

        @pl.when((step > 0) & (step <= chunks))
        def _():
            c = step - 1
            cols = span(c, tile)

            @pl.loop(1, experts)
            def _(k):
                back_copy(c, lax.rem(me + k, experts), me).wait_recv()

            block = returned[:, cols]
            value = (
                tokens[:, cols].astype(jnp.float32)
                + jnp.dot(weight_hi[...], block, preferred_element_type=jnp.float32)
                + jnp.dot(weight_lo[...], block, preferred_element_type=jnp.float32)
            ).astype(jnp.bfloat16)
            moe_out[:, cols] = value
            encoded[:, cols] = value
            encoded_all[span(me, rows), cols] = value
            plane_start(second, c)

        @pl.when(step > 1)
        def _():
            plane_relay(second, step - 2)

    @pl.loop(0, chunks)
    def _(c):
        plane_arrive(second, c)

    @pl.loop(0, chunks)
    def _(c):
        plane_finish(first, c)
        plane_finish(second, c)

        @pl.loop(1, experts)
        def _(k):
            back_copy(c, me, lax.rem(me + k, experts)).wait_send()

    @pl.loop(0, n)
    def _(g):
        @pl.loop(0, chunks)
        def _(c):
            @pl.when((g <= p) & (p < n - 1))
            def _():
                z_copy(g, c, 0, p).wait_send()

            @pl.when((g >= p) & (p > 0))
            def _():
                z_copy(g, c, 1, p).wait_send()

            @pl.when(g != p)
            def _():
                rs_copy(g, c, g, p).wait_send()


def kv_kernel(moe_all, gain, weight, out, encoded):
    rows, width = moe_all.shape
    step = 128

    @pl.loop(0, rows // step)
    def _(i):
        piece = pl.ds(pl.multiple_of(i * step, step), step)
        encoded[piece] = normalize(moe_all[piece].astype(jnp.float32), gain[...]).astype(jnp.bfloat16)

    @pl.loop(0, weight.shape[0] // step)
    def _(i):
        piece = pl.ds(pl.multiple_of(i * step, step), step)
        out[piece] = lax.dot_general(
            weight[piece], encoded[...], (((1,), (1,)), ((), ())), preferred_element_type=jnp.float32
        ).astype(jnp.bfloat16)


def local(
    tokens,
    norm_gain,
    router_weight,
    gate_weight,
    up_weight,
    down_weight,
    expert_picks,
    final_gain,
    kv_weight,
):
    n = lax.axis_size("dp")
    experts = lax.axis_size("expert")
    me = lax.axis_index("expert")
    rows, width = tokens.shape
    ff = gate_weight.shape[2]
    chosen = expert_picks[0]
    cap = chosen.shape[1]
    slots = 4 * rows // experts
    wide_tokens = tokens.astype(jnp.float32)
    normed = normalize(wide_tokens, norm_gain).astype(jnp.bfloat16)
    gate_probs = jax.nn.sigmoid(jnp.dot(normed, router_weight, preferred_element_type=jnp.float32))
    source = chosen // rows
    local_row = chosen % rows
    positions = jnp.arange(cap, dtype=jnp.int32)
    earlier = (source[:, :, None] == source[:, None, :]) & (
        positions[None, None, :] < positions[None, :, None]
    )
    slot_rank = jnp.sum(earlier.astype(jnp.int32), axis=2)
    own_chosen = lax.dynamic_index_in_dim(chosen, me, 0, keepdims=False)
    own_rank = lax.dynamic_index_in_dim(slot_rank, me, 0, keepdims=False)
    own_slot = (own_chosen // rows) * slots + own_rank
    pick_map = (own_chosen[:, None] == jnp.arange(experts * rows, dtype=jnp.int32)[None, :]).astype(jnp.bfloat16)
    out_map = (jnp.arange(experts * slots, dtype=jnp.int32)[:, None] == own_slot[None, :]).astype(jnp.bfloat16)
    send_slot = (
        (source == me)[:, :, None] & (slot_rank[:, :, None] == jnp.arange(slots, dtype=jnp.int32))
    ).astype(jnp.bfloat16)
    local_map = (local_row[:, :, None] == jnp.arange(rows, dtype=jnp.int32)).astype(jnp.bfloat16)
    send_map = jnp.einsum("ecm,ect->tem", send_slot, local_map, preferred_element_type=jnp.float32)
    weight = (send_map * gate_probs[:, :, None]).reshape(rows, experts * slots)
    weight_hi = lax.reduce_precision(weight, 8, 7)
    weight_lo = (weight - weight_hi).astype(jnp.bfloat16)
    weight_hi = weight_hi.astype(jnp.bfloat16)

    chunks = 4
    bf16 = jnp.bfloat16
    dma = pltpu.SemaphoreType.DMA
    vmem = pl.BlockSpec(memory_space=pltpu.VMEM)
    hbm = pl.BlockSpec(memory_space=pl.ANY)
    moe_out, moe_all = pl.pallas_call(
        functools.partial(kernel, n, experts, chunks),
        out_shape=(
            jax.ShapeDtypeStruct((rows, width), bf16),
            jax.ShapeDtypeStruct((experts * rows, width), bf16),
        ),
        in_specs=[vmem] * 6 + [hbm] * 3,
        out_specs=(vmem, vmem),
        scratch_shapes=[
            pltpu.VMEM((width, ff), bf16),
            pltpu.VMEM((width, ff), bf16),
            pltpu.VMEM((ff, width), bf16),
            pltpu.VMEM((experts * rows, width), bf16),
            pltpu.VMEM((n, cap, width), bf16),
            pltpu.VMEM((cap, ff), bf16),
            pltpu.VMEM((n, cap, width), bf16),
            pltpu.VMEM((n + 1, cap, width), bf16),
            pltpu.VMEM((experts * slots, width), bf16),
            pltpu.VMEM((experts * slots, width), bf16),
            pltpu.VMEM((rows, width), bf16),
            dma((3,)),
            dma((experts, chunks)),
            dma((experts, chunks)),
            dma((2, n, chunks)),
            dma((n, chunks)),
            dma((n, chunks)),
            dma((n + 1, chunks)),
            dma((experts, chunks)),
            dma((experts, chunks)),
            dma((experts, chunks)),
            dma((experts, chunks)),
        ],
        compiler_params=pltpu.CompilerParams(
            collective_id=0, has_side_effects=True, vmem_limit_bytes=60 * 1024 * 1024
        ),
    )(
        normed, tokens, pick_map, out_map, weight_hi, weight_lo,
        gate_weight, up_weight, down_weight,
    )
    all_rows = moe_all.shape[0]
    kv_matrix = kv_weight.reshape(width, -1).T
    kv_rows = pl.pallas_call(
        kv_kernel,
        out_shape=jax.ShapeDtypeStruct((kv_matrix.shape[0], all_rows), bf16),
        in_specs=[vmem] * 3,
        out_specs=vmem,
        scratch_shapes=[pltpu.VMEM((all_rows, width), bf16)],
        compiler_params=pltpu.CompilerParams(vmem_limit_bytes=40 * 1024 * 1024),
    )(moe_all, final_gain[None, :], kv_matrix)
    kv_cache = kv_rows.T.reshape((all_rows,) + kv_weight.shape[1:])
    return (moe_out, kv_cache)


def solution(mesh):
    in_specs = (
        P(("dp", "expert"), None),
        P(),
        P(),
        P("expert", None, "dp"),
        P("expert", None, "dp"),
        P("expert", "dp", None),
        P("dp", None, None),
        P(),
        P(None, "expert", None, None, None),
    )
    out_specs = (P(("dp", "expert"), None), P("dp", "expert", None, None, None))
    return jax.shard_map(local, mesh=mesh, in_specs=in_specs, out_specs=out_specs, check_vma=False)
```

time: 142 us -> 124 us (0.87)
  Pallas kernels: 119 us -> 111 us
  matrix products: 6.22 us -> 0.38 us
  local copies, waits for them, and re-layouts: 7.86 us -> 3.8 us
    pallas_call x1, Pallas kernels: 119 us -> 104 us  [local(): pl.pallas_call(functools.partial(kernel, n, experts, chunks), out_shape=(...]
    pallas_call x0 -> x1, Pallas kernels: none -> 6.73 us  [local(): pl.pallas_call(kv_kernel, out_shape=jax.ShapeDtypeStruct((kv_matrix.shape...]
    dot_general x1 -> x0, matrix products: 4.4 us -> none  [local(): lax.dot_general(kv_matrix, encoded_all, (((0,), (1,)), ((), ())), preferr...]
    convert_element_type x1 -> x0, local copies, waits for them, and re-layouts: 2.29 us -> none  [local(): kv_rows = lax.dot_general(kv_matrix, encoded_all, (((0,), (1,)), ((), ())...]
where the time goes in v2:
time: 124 us; the launch traced here: 123 us
  Pallas kernels  111 us (90%)
  other arithmetic  7.38 us (6%)
  local copies, waits for them, and re-layouts  3.8 us (3%)
    pallas_call x1, Pallas kernels, local(): pl.pallas_call(functools.partial(kernel, n, experts, chunks), out_shape=(...  104 us
    pallas_call x1, Pallas kernels, local(): pl.pallas_call(kv_kernel, out_shape=jax.ShapeDtypeStruct((kv_matrix.shape...  6.73 us

profile of v2, /device:TPU:0, one launch (start us, length us, event | category | flops | bytes accessed | tf_op | source)
XLA Modules:
  0.0 123.3 jit_solution(3612351678994554258)
XLA Ops:
  0.6 0.0 copy-start
  0.6 1.1 fusion.4
  1.8 0.7 fusion.18
  2.5 0.7 add_select_fusion
  3.2 0.7 broadcast_compare_fusion
  3.9 0.7 convert_element_type.27
  4.6 0.7 broadcast_in_dim.2.gain
  5.3 0.4 convert_reduce_fusion
  5.6 0.7 add_bitcast_fusion
  6.3 0.6 fusion.9.out_map
  7.0 0.7 fusion.7.pick_map
  7.7 1.1 fusion.6.normed
  8.8 0.0 copy-done
  8.8 0.0 copy-start.3
  8.8 0.2 fusion.3
  9.0 0.2 fusion
  9.2 0.1 copy.14
  9.3 0.6 fusion.12
  9.9 0.0 copy-done.3
  10.0 0.0 copy-start.1
  10.0 104.3 %shard_map.104 = (bf16[64,2048]{1,0:T(8,128)(2,1)}, bf16[512,2048]{1,0:T(8,128)(2,1)}) custom-call(bf16[64,2048]{1,0:T(8,128)(2,1)} %copy-done.3, bf16[64,2048]{1,0:T(8,128)(2,1)} %tokens.1, bf16[128,512]{1,0:T(8,128)(2,1)} %fusion.7.pick_map, bf16[256,128]{1,0:T(8,128)(2,1)} %fusion.9.out_map, bf16[64,256]{1,0:T(8,128)(2,1)} %get-tuple-element.9.weight_hi, ...), custom_call_target="tpu_custom_call" | custom-call | tf_op jit(solution)/shard_map/pallas_call | solution.py:392
  114.2 0.0 copy-done.1
  114.2 0.0 copy-start.2
  114.2 1.6 %copy-done.2 = bf16[512,2048]{1,0:T(8,128)(2,1)S(1)} copy-done((bf16[512,2048]{1,0:T(8,128)(2,1)S(1)}, bf16[512,2048]{1,0:T(8,128)(2,1)}, u32[]{:S(2)}) %copy-start.2) | copy-done | bytes 2097176
  115.8 0.0 copy-start.4
  115.8 6.7 %shard_map.105 = bf16[768,512]{1,0:T(8,128)(2,1)} custom-call(bf16[512,2048]{1,0:T(8,128)(2,1)S(1)} %copy-done.2, bf16[1,2048]{1,0:T(2,128)(2,1)S(1)} %broadcast_in_dim.2.gain, bf16[768,2048]{1,0:T(8,128)(2,1)S(1)} %bitcast.54), custom_call_target="tpu_custom_call" | custom-call | tf_op jit(solution)/shard_map/pallas_call | solution.py:433
  122.6 0.0 copy-done.4
  122.6 0.7 copy.17
  (2 shorter events, 0.0 us)
Async XLA Ops:
  0.6 8.2 %copy-start = (bf16[2048,8]{0,1:T(8,128)(2,1)S(1)}, bf16[2048,8]{0,1:T(8,128)(2,1)}, u32[]{:S(2)}) copy-start(bf16[2048,8]{0,1:T(8,128)(2,1)} %param.11) | copy-start | bytes 98308
  8.8 1.1 copy-start.3
  10.0 104.3 %copy-start.1 = (bf16[2048,1,6,2,64]{0,4,3,2,1:T(8,128)(2,1)S(1)}, bf16[2048,1,6,2,64]{0,4,3,2,1:T(8,128)(2,1)}, u32[]{:S(2)}) copy-start(bf16[2048,1,6,2,64]{0,4,3,2,1:T(8,128)(2,1)} %param.17) | copy-start | bytes 9437188
  114.2 1.6 %copy-start.2 = (bf16[512,2048]{1,0:T(8,128)(2,1)S(1)}, bf16[512,2048]{1,0:T(8,128)(2,1)}, u32[]{:S(2)}) copy-start(bf16[512,2048]{1,0:T(8,128)(2,1)} %get-tuple-element.5.moe_all) | copy-start | bytes 6291460
  115.8 6.7 %copy-start.4 = (bf16[64,2048]{1,0:T(8,128)(2,1)S(1)}, bf16[64,2048]{1,0:T(8,128)(2,1)}, u32[]{:S(2)}) copy-start(bf16[64,2048]{1,0:T(8,128)(2,1)} %get-tuple-element.12) | copy-start | bytes 786436
